TPU v7x, 32 devices: a whole 2x2x4 slice. The times are simulated.
32 devices in a mesh: sp: 8 (over z, y), tp: 4 (over x, core).
Axes of the slice: x: 2, y: 2, z: 4, core: 2. Of those that a mesh axis runs over, the one named last changes fastest.
Arguments:
- decay_rate: float32 [4, 8192, 1024], P(None, 'sp', 'tp'), may hold values from 0.2 to 2
- drive_in: bfloat16 [4, 8192, 1024], P(None, 'sp', 'tp'), may hold values from -6 to 6
- gate_in: bfloat16 [4, 8192, 1024], P(None, 'sp', 'tp'), may hold values from -6 to 6
- norm_gain: float32 [1024], P('tp'), may hold values from 0.25 to 1.75
Outputs:
- filtered: bfloat16 [4, 8192, 1024], P(None, 'sp', 'tp')
All inputs are finite; a program needn't handle non-finite values.
Results may differ from a plain program's by a relative error of at most 0.0015.
Values sent between devices are 32-bit elements.
A program may use at most 128 MiB of HBM per device.

v0:
```python
import jax
import jax.numpy as jnp
from jax import lax
from jax.sharding import PartitionSpec as P


def carried_in(part, axis, combine, identity):
    place = lax.axis_index(axis)
    gathered = jax.tree.map(lambda a: lax.all_gather(a, axis), part)
    state = jax.tree.map(lambda a, e: jnp.zeros_like(a) + jnp.asarray(e, a.dtype), part, identity)

    def one(step, state):
        return combine(
            state, jax.tree.map(lambda a: lax.dynamic_index_in_dim(a, step, 0, False), gathered)
        )

    return lax.fori_loop(0, place, one, state)


def join_pair(earlier, later):
    return (earlier[0] * later[0], later[0] * earlier[1] + later[1])


def shards(decay_rate, drive_in, gate_in, norm_gain):
    total_length = decay_rate.shape[1] * lax.axis_size("sp")
    keep = jnp.exp(-decay_rate / total_length)
    push = drive_in.astype(jnp.float32) * total_length ** (-0.5)
    steps = -decay_rate / total_length
    logs = jnp.sum(steps, axis=1, keepdims=True) - jnp.cumsum(steps, axis=1)
    summary = (jnp.exp(jnp.sum(steps, axis=1)), jnp.sum(jnp.exp(logs) * push, axis=1))
    entering_forward = carried_in(
        summary, "sp", join_pair, (jnp.ones_like(keep[:, 0]), jnp.zeros_like(push[:, 0]))
    )
    started = push.at[:, 0].add(keep[:, 0] * entering_forward[1])
    forward = lax.associative_scan(join_pair, (keep, started), axis=1)[1]
    gated = forward * jax.nn.sigmoid(gate_in.astype(jnp.float32))
    power = lax.psum(jnp.sum(gated * gated, axis=-1, keepdims=True), "tp") / (
        gated.shape[-1] * lax.axis_size("tp")
    )
    filtered = (gated * lax.rsqrt(power + 1e-06) * norm_gain).astype(jnp.bfloat16)
    return filtered


def solution(mesh):
    placed = (P(None, "sp", "tp"), P(None, "sp", "tp"), P(None, "sp", "tp"), P("tp"))
    return jax.shard_map(
        shards, mesh=mesh, in_specs=placed, out_specs=P(None, "sp", "tp"), check_vma=False
    )
```

profile of v0, /device:TPU:0, one launch (start us, length us, event | category | flops | bytes accessed | tf_op | source)
XLA Modules:
  0.0 258.0 jit_solution(10280227825834792261)
XLA Ops:
  0.0 2.9 %fusion.17 = (f32[4,1024,256]{2,1,0:T(8,128)S(1)}, f32[4,256]{1,0:T(4,128)S(1)}, f32[4,1024,256]{2,1,0:T(8,128)S(1)}) fusion(f32[4,1024,256]{2,1,0:T(8,128)} %param.8), kind=kLoop, calls=%fused_computation.64 | loop fusion | flops 3144704 | bytes 12587008 | tf_op jit(solution)/shard_map/exp | solution.py:26
  5.6 32.4 %all-gather.2 = f32[8,4,256]{2,1,0:T(4,128)S(1)} all-gather(f32[1,4,256]{2,1,0:T(4,128)S(1)} %exponential_bitcast_fusion), channel_id=2, replica_groups=mesh['sp'=8,'tp'=4] {'sp'}, dimensions={0}, use_global_device_ids=true | all-gather | bytes 36864 | tf_op jit(solution)/shard_map/all_gather | solution.py:9
  42.3 3.2 %fusion = (f32[4,256]{1,0:T(4,128)S(1)}, f32[4,1024,256]{2,1,0:T(8,128)}) fusion(f32[4,256,8,128]{1,3,2,0:T(8,128)S(1)} %copy.18, f32[4,256]{1,0:T(4,128)S(1)} %get-tuple-element.75, bf16[4,1024,256]{2,1,0:T(8,128)(2,1)S(1)} %copy-done.5), kind=kLoop, calls=%fused_computation.3 | loop fusion | flops 5241856 | bytes 10493952 | tf_op jit(solution)/shard_map/reduce_sum | solution.py:30
  45.5 30.6 %all-gather.3 = f32[8,4,256]{2,1,0:T(4,128)S(1)} all-gather(f32[1,4,256]{2,1,0:T(4,128)S(1)} %bitcast.63), channel_id=3, replica_groups=mesh['sp'=8,'tp'=4] {'sp'}, dimensions={0}, use_global_device_ids=true | all-gather | bytes 36864 | tf_op jit(solution)/shard_map/all_gather | solution.py:9
  78.3 11.9 %slice.337 = f32[4,511,256]{2,1,0:T(8,128)} slice(f32[4,1024,256]{2,1,0:T(8,128)} %scatter-add.4), slice={[0:4:1], [2:1024:2], [0:256:1]} | slice | bytes 4186112 | tf_op jit(solution)/shard_map/slice | solution.py:35
  90.2 11.8 %slice.267 = f32[4,512,256]{2,1,0:T(8,128)} slice(f32[4,1024,256]{2,1,0:T(8,128)} %scatter-add.4), slice={[0:4:1], [1:1024:2], [0:256:1]} | slice | bytes 4194304 | tf_op jit(solution)/shard_map/slice | solution.py:35
  102.0 11.7 %slice.266 = f32[4,512,256]{2,1,0:T(8,128)} slice(f32[4,1024,256]{2,1,0:T(8,128)} %scatter-add.4), slice={[0:4:1], [0:1023:2], [0:256:1]} | slice | bytes 4194304 | tf_op jit(solution)/shard_map/slice | solution.py:35
  113.7 11.8 %slice.269 = f32[4,512,256]{2,1,0:T(8,128)} slice(f32[4,1024,256]{2,1,0:T(8,128)} %copy-done), slice={[0:4:1], [0:1023:2], [0:256:1]} | slice | bytes 4194304 | tf_op jit(solution)/shard_map/slice | solution.py:35
  125.5 11.8 %slice.265 = f32[4,512,256]{2,1,0:T(8,128)} slice(f32[4,1024,256]{2,1,0:T(8,128)} %copy-done), slice={[0:4:1], [1:1024:2], [0:256:1]} | slice | bytes 4194304 | tf_op jit(solution)/shard_map/slice | solution.py:35
  137.3 5.4 %fusion.18 = (f32[4,512,256]{2,1,0:T(8,128)}, f32[4,512,256]{2,1,0:T(8,128)S(1)}) fusion(f32[4,512,256]{2,1,0:T(8,128)} %slice.269, f32[4,512,256]{2,1,0:T(8,128)} %slice.265, f32[4,512,256]{2,1,0:T(8,128)} %slice.267, f32[4,512,256]{2,1,0:T(8,128)} %slice.266), kind=kLoop, calls=%fused_computation.65 | loop fusion | flops 1572864 | bytes 12582912 | tf_op jit(solution)/shard_map/mul | solution.py:21
  142.7 11.9 %slice.264 = f32[4,511,256]{2,1,0:T(8,128)} slice(f32[4,1024,256]{2,1,0:T(8,128)} %copy-done), slice={[0:4:1], [2:1024:2], [0:256:1]} | slice | bytes 4186112 | tf_op jit(solution)/shard_map/slice | solution.py:35
  154.6 7.3 %slice.275 = f32[4,256,256]{2,1,0:T(8,128)} slice(f32[4,512,256]{2,1,0:T(8,128)} %get-tuple-element.77), slice={[0:4:1], [0:511:2], [0:256:1]} | slice | bytes 2097152 | tf_op jit(solution)/shard_map/slice | solution.py:35
  161.9 7.3 %slice.271 = f32[4,256,256]{2,1,0:T(8,128)} slice(f32[4,512,256]{2,1,0:T(8,128)} %get-tuple-element.77), slice={[0:4:1], [1:512:2], [0:256:1]} | slice | bytes 2097152 | tf_op jit(solution)/shard_map/slice | solution.py:35
  169.2 6.0 %slice.270 = f32[4,255,256]{2,1,0:T(8,128)S(1)} slice(f32[4,512,256]{2,1,0:T(8,128)} %get-tuple-element.77), slice={[0:4:1], [2:512:2], [0:256:1]} | slice | bytes 2088960 | tf_op jit(solution)/shard_map/slice | solution.py:35
  175.3 4.2 %slice.335 = f32[4,255,256]{2,1,0:T(8,128)} slice(f32[4,512,256]{2,1,0:T(8,128)S(1)} %get-tuple-element.78), slice={[0:4:1], [2:512:2], [0:256:1]} | slice | bytes 2088960 | tf_op jit(solution)/shard_map/slice | solution.py:35
  179.5 4.2 %slice.273 = f32[4,256,256]{2,1,0:T(8,128)} slice(f32[4,512,256]{2,1,0:T(8,128)S(1)} %get-tuple-element.78), slice={[0:4:1], [1:512:2], [0:256:1]} | slice | bytes 2097152 | tf_op jit(solution)/shard_map/slice | solution.py:35
  183.7 4.2 %slice.272 = f32[4,256,256]{2,1,0:T(8,128)} slice(f32[4,512,256]{2,1,0:T(8,128)S(1)} %get-tuple-element.78), slice={[0:4:1], [0:511:2], [0:256:1]} | slice | bytes 2097152 | tf_op jit(solution)/shard_map/slice | solution.py:35
  211.9 3.3 %pad.80 = f32[4,512,256]{2,1,0:T(8,128)} pad(f32[4,256,256]{2,1,0:T(8,128)S(1)} %add.184, f32[]{:T(128)} %constant.60.clone.1), padding=0_0_0x1_0_1x0_0_0 | pad | bytes 3145732 | tf_op jit(solution)/shard_map/pad | solution.py:35
  215.2 3.5 %fusion.4 = f32[4,511,256]{2,1,0:T(8,128)S(1)} fusion(f32[4,511,256]{2,1,0:T(8,128)} %slice.337, f32[4,511,256]{2,1,0:T(8,128)} %slice.264, f32[4,512,256]{2,1,0:T(8,128)} %pad.80, f32[4,512,256]{2,1,0:T(8,128)S(1)} %pad.79), kind=kLoop, calls=%fused_computation.14 | loop fusion | flops 1569792 | bytes 10465280 | tf_op jit(solution)/shard_map/add | solution.py:21
  221.8 9.4 %pad.81 = f32[4,1024,256]{2,1,0:T(8,128)} pad(f32[4,512,256]{2,1,0:T(8,128)} %pad_maximum_fusion, f32[]{:T(128)} %constant.60.clone.1), padding=0_0_0x0_1_1x0_0_0 | pad | bytes 6291460 | tf_op jit(solution)/shard_map/pad | solution.py:35
  231.2 5.8 %pad.82 = f32[4,1024,256]{2,1,0:T(8,128)} pad(f32[4,512,256]{2,1,0:T(8,128)S(1)} %copy-done.3, f32[]{:T(128)} %constant.60.clone.1), padding=0_0_0x1_0_1x0_0_0 | pad | bytes 6291460 | tf_op jit(solution)/shard_map/pad | solution.py:35
  237.1 7.3 %multiply_reduce_fusion = (f32[4,1024]{1,0:T(4,128)S(1)}, f32[4,1024,256]{2,1,0:T(8,128)}) fusion(bf16[4,1024,256]{2,1,0:T(8,128)(2,1)} %param.10, f32[4,1024,256]{2,1,0:T(8,128)} %pad.81, f32[4,1024,256]{2,1,0:T(8,128)} %pad.82), kind=kLoop, calls=%fused_computation.9 | loop fusion | flops 8384512 | bytes 14696448 | tf_op jit(solution)/shard_map/reduce_sum | solution.py:37
  244.3 10.1 %psum.7 = f32[4,1024,1]{1,0,2:T(4,128)S(1)} all-reduce(f32[4,1024,1]{1,0,2:T(4,128)S(1)} %bitcast.58), channel_id=1, replica_groups=mesh['sp'=8,'tp'=4] {'tp'}, use_global_device_ids=true, to_apply=%region_7.8 | all-reduce | flops 4096 | bytes 32768 | tf_op jit(solution)/shard_map/psum | solution.py:37
  254.5 3.6 %multiply_convert_fusion = bf16[4,1024,256]{2,1,0:T(8,128)(2,1)} fusion(f32[4,1024,256]{2,1,0:T(8,128)} %get-tuple-element.73, f32[256]{0:T(256)S(1)} %copy-done.6, f32[4,1024]{1,0:T(4,128)S(1)} %rsqrt_bitcast_fusion), kind=kLoop, calls=%fused_computation.8 | loop fusion | flops 3145728 | bytes 6308864 | tf_op jit(solution)/shard_map/convert_element_type | solution.py:40
  (125 shorter events, 35.7 us)
Async XLA Ops:
  3.0 2.6 %copy-start = (f32[4,1024,256]{2,1,0:T(8,128)}, f32[4,1024,256]{2,1,0:T(8,128)S(1)}, u32[]{:S(2)}) copy-start(f32[4,1024,256]{2,1,0:T(8,128)S(1)} %get-tuple-element.74) | copy-start | bytes 12582916
  5.6 32.5 %copy-start.2 = (f32[4,256,8,128]{1,2,3,0:T(8,128)}, f32[4,256,8,128]{1,2,3,0:T(8,128)S(1)}, u32[]{:S(2)}) copy-start(f32[4,256,8,128]{1,2,3,0:T(8,128)S(1)} %fusion.2) | copy-start | bytes 12582916
  40.7 1.6 copy-start.5
  202.1 1.4 copy-start.4
  215.2 3.5 %copy-start.1 = (f32[4,512,256]{2,1,0:T(8,128)S(1)}, f32[4,512,256]{2,1,0:T(8,128)}, u32[]{:S(2)}) copy-start(f32[4,512,256]{2,1,0:T(8,128)} %pad.80) | copy-start | bytes 6291460
  221.8 9.4 %copy-start.3 = (f32[4,512,256]{2,1,0:T(8,128)S(1)}, f32[4,512,256]{2,1,0:T(8,128)}, u32[]{:S(2)}) copy-start(f32[4,512,256]{2,1,0:T(8,128)} %add.186) | copy-start | bytes 6291460
  237.1 17.4 %copy-start.6 = (f32[256]{0:T(256)S(1)}, f32[256]{0:T(256)}, u32[]{:S(2)}) copy-start(f32[256]{0:T(256)} %param.11) | copy-start | bytes 3076
where the time goes:
time: 261 us; the launch traced here: 258 us
  local copies, waits for them, and re-layouts  140 us (54%)
  blocking collectives  73.1 us (28%)
  other arithmetic  44.3 us (17%)
    slice x59, local copies, waits for them, and re-layouts, shards(): forward = lax.associative_scan(join_pair, (keep, started), axis=1)[1]  113 us
    all_gather x2, blocking collectives, carried_in(): gathered = jax.tree.map(lambda a: lax.all_gather(a, axis), part)  63 us
    pad x18, local copies, waits for them, and re-layouts, shards(): forward = lax.associative_scan(join_pair, (keep, started), axis=1)[1]  23.8 us
    mul x8, other arithmetic, join_pair(): return (earlier[0] * later[0], later[0] * earlier[1] + later[1])  10.5 us
    psum x1, blocking collectives, shards(): lax.psum(jnp.sum(gated * gated, axis=-1, keepdims=True), 'tp')  10.1 us
    reduce_sum x1, other arithmetic, shards(): jnp.sum(gated * gated, axis=-1, keepdims=True)  7.26 us
    add x9, other arithmetic, join_pair(): return (earlier[0] * later[0], later[0] * earlier[1] + later[1])  5.34 us
    another operation x4, other arithmetic  5.26 us

commit v1 on v0

v1 whole, which is shorter than its diff:
```python
import functools

import jax
import jax.numpy as jnp
from jax import lax
from jax.experimental import pallas as pl
from jax.experimental.pallas import tpu as pltpu
from jax.sharding import PartitionSpec as P

CHUNK = 128
MESH = pl.DeviceIdType.MESH


def split(x):
    high = x.astype(jnp.bfloat16)
    low = (x - high.astype(jnp.float32)).astype(jnp.bfloat16)
    return jnp.concatenate([high, low], axis=0)


def kernel(
    n_sp, n_tp, total_length, decay_hbm, drive_hbm, gate_hbm, gain_ref, out_hbm,
    decay, drive, gate, sums, out, chunk_keep, chunk_state,
    mine, gathered, my_power, powers,
    in_sem, out_sem, sp_send, sp_recv, tp_send, tp_recv,
):
    batch, length, channels = decay.shape
    chunks = length // CHUNK
    sp, tp = lax.axis_index("sp"), lax.axis_index("tp")

    def load(b, which):
        src, dst = ((decay_hbm, decay), (drive_hbm, drive), (gate_hbm, gate))[which]
        return pltpu.make_async_copy(src.at[b], dst.at[b], in_sem.at[which, b])

    def store(b):
        return pltpu.make_async_copy(out.at[b], out_hbm.at[b], out_sem.at[b])

    def to_later(j, b):
        return pltpu.make_async_remote_copy(
            src_ref=mine.at[b], dst_ref=gathered.at[sp, b],
            send_sem=sp_send.at[j, b], recv_sem=sp_recv.at[sp, b],
            device_id={"sp": j}, device_id_type=MESH,
        )

    def from_earlier(j, b):
        return pltpu.make_async_remote_copy(
            src_ref=mine.at[b], dst_ref=gathered.at[j, b],
            send_sem=sp_send.at[j, b], recv_sem=sp_recv.at[j, b],
            device_id={"sp": j}, device_id_type=MESH,
        )

    def to_peer(i, b):
        return pltpu.make_async_remote_copy(
            src_ref=my_power.at[b], dst_ref=powers.at[i - 1, b],
            send_sem=tp_send.at[i - 1, b], recv_sem=tp_recv.at[i - 1, b],
            device_id={"tp": lax.rem(tp + i, n_tp)}, device_id_type=MESH,
        )

    for b in range(batch):
        load(b, 0).start()
        load(b, 1).start()
    for b in range(batch):
        load(b, 2).start()

    barrier = pltpu.get_barrier_semaphore()

    def greet(j, _):
        pl.semaphore_signal(barrier, inc=1, device_id={"sp": j}, device_id_type=MESH)
        return 0

    lax.fori_loop(0, sp, greet, 0)
    for i in range(1, n_tp):
        pl.semaphore_signal(
            barrier, inc=1, device_id={"tp": lax.rem(tp + i, n_tp)}, device_id_type=MESH
        )

    row = lax.broadcasted_iota(jnp.int32, (CHUNK, 2 * CHUNK), 0)
    column = lax.broadcasted_iota(jnp.int32, (CHUNK, 2 * CHUNK), 1)
    column = jnp.where(column >= CHUNK, column - CHUNK, column)
    lower = jnp.where(column <= row, 1.0, 0.0).astype(jnp.bfloat16)

    def running(x):
        return jnp.dot(lower, split(x), preferred_element_type=jnp.float32)

    def scan_batch(b, _):
        load(b, 0).wait()
        load(b, 1).wait()
        keep = jnp.ones((1, channels), jnp.float32)
        state = jnp.zeros((1, channels), jnp.float32)
        for k in range(chunks):
            at = pl.ds(k * CHUNK, CHUNK)
            passed = running(decay[b, at]) * (1.0 / total_length)
            summed = running(jnp.exp(passed) * drive[b, at].astype(jnp.float32))
            fall = jnp.exp(-passed)
            decay[b, at] = fall
            sums[b, at] = summed
            chunk_keep[b, pl.ds(k, 1)] = keep
            chunk_state[b, pl.ds(k, 1)] = state
            last = fall[CHUNK - 1 :]
            state = last * (state + summed[CHUNK - 1 :])
            keep = last * keep
        mine[b, pl.ds(0, 1)] = keep
        mine[b, pl.ds(1, 1)] = state

        @pl.when(b == 0)
        def _():
            pl.semaphore_wait(barrier, n_sp - 1 - sp + n_tp - 1)

        def send(i, _):
            to_later(n_sp - 1 - i, b).start()
            return 0

        lax.fori_loop(0, n_sp - 1 - sp, send, 0)
        return 0

    lax.fori_loop(0, batch, scan_batch, 0)

    def gate_batch(b, _):
        load(b, 2).wait()
        for k in range(chunks):
            at = pl.ds(k * CHUNK, CHUNK)
            opened = decay[b, at] * (1.0 + jnp.tanh(0.5 * gate[b, at].astype(jnp.float32)))
            decay[b, at] = opened
            sums[b, at] = opened * sums[b, at]
        return 0

    lax.fori_loop(0, batch, gate_batch, 0)

    lane = lax.broadcasted_iota(jnp.int32, (CHUNK, CHUNK), 1)

    def join_batch(b, _):
        def earlier(j, state):
            from_earlier(j, b).wait_recv()
            return gathered[j, b, pl.ds(0, 1)] * state + gathered[j, b, pl.ds(1, 1)]

        entering = lax.fori_loop(0, sp, earlier, jnp.zeros((1, channels), jnp.float32))
        states = chunk_keep[b] * entering + chunk_state[b]
        squares = jnp.zeros((CHUNK, CHUNK), jnp.float32)
        for k in range(chunks):
            at = pl.ds(k * CHUNK, CHUNK)
            gated = decay[b, at] * states[k : k + 1] + sums[b, at]
            sums[b, at] = gated
            squares = jnp.where(lane == k, jnp.sum(gated * gated, axis=1, keepdims=True), squares)
        my_power[b] = jnp.transpose(squares)[:chunks]
        for i in range(1, n_tp):
            to_peer(i, b).start()
        return 0

    lax.fori_loop(0, batch, join_batch, 0)

    gain = gain_ref[...]

    def norm_batch(b, _):
        power = my_power[b]
        for i in range(1, n_tp):
            to_peer(i, b).wait_recv()
            power = power + powers[i - 1, b]
        scale = lax.rsqrt(power / (channels * n_tp) + 4e-6 * total_length)
        scale = jnp.transpose(
            jnp.concatenate([scale, jnp.zeros((CHUNK - chunks, CHUNK), jnp.float32)], axis=0)
        )
        for k in range(chunks):
            at = pl.ds(k * CHUNK, CHUNK)
            out[b, at] = (sums[b, at] * scale[:, k : k + 1] * gain).astype(jnp.bfloat16)
        store(b).start()
        return 0

    lax.fori_loop(0, batch, norm_batch, 0)

    for b in range(batch):
        store(b).wait()

        def sent(i, _):
            to_later(n_sp - 1 - i, b).wait_send()
            return 0

        lax.fori_loop(0, n_sp - 1 - sp, sent, 0)
        for i in range(1, n_tp):
            to_peer(i, b).wait_send()


def solution(mesh):
    n_sp, n_tp = mesh.shape["sp"], mesh.shape["tp"]

    def shards(decay_rate, drive_in, gate_in, norm_gain):
        batch, length, channels = decay_rate.shape
        chunks = length // CHUNK
        f32 = jnp.float32
        return pl.pallas_call(
            functools.partial(kernel, n_sp, n_tp, length * n_sp),
            out_shape=jax.ShapeDtypeStruct((batch, length, channels), jnp.bfloat16),
            in_specs=[pl.BlockSpec(memory_space=pl.ANY)] * 3
            + [pl.BlockSpec(memory_space=pltpu.VMEM)],
            out_specs=pl.BlockSpec(memory_space=pl.ANY),
            scratch_shapes=[
                pltpu.VMEM((batch, length, channels), f32),
                pltpu.VMEM((batch, length, channels), jnp.bfloat16),
                pltpu.VMEM((batch, length, channels), jnp.bfloat16),
                pltpu.VMEM((batch, length, channels), f32),
                pltpu.VMEM((batch, length, channels), jnp.bfloat16),
                pltpu.VMEM((batch, chunks, channels), f32),
                pltpu.VMEM((batch, chunks, channels), f32),
                pltpu.VMEM((batch, 2, channels), f32),
                pltpu.VMEM((n_sp, batch, 2, channels), f32),
                pltpu.VMEM((batch, chunks, CHUNK), f32),
                pltpu.VMEM((n_tp - 1, batch, chunks, CHUNK), f32),
                pltpu.SemaphoreType.DMA((3, batch)),
                pltpu.SemaphoreType.DMA((batch,)),
                pltpu.SemaphoreType.DMA((n_sp, batch)),
                pltpu.SemaphoreType.DMA((n_sp, batch)),
                pltpu.SemaphoreType.DMA((n_tp - 1, batch)),
                pltpu.SemaphoreType.DMA((n_tp - 1, batch)),
            ],
            compiler_params=pltpu.CompilerParams(collective_id=0, has_side_effects=True),
        )(decay_rate, drive_in, gate_in, norm_gain.reshape(1, channels))

    placed = (P(None, "sp", "tp"), P(None, "sp", "tp"), P(None, "sp", "tp"), P("tp"))
    return jax.shard_map(
        shards, mesh=mesh, in_specs=placed, out_specs=P(None, "sp", "tp"), check_vma=False
    )
```

time: 261 us -> 19.8 us (0.08); the launches traced: 258 us -> 19.7 us
  local copies, waits for them, and re-layouts: 140 us -> 3.05 us
  blocking collectives: 73.1 us -> 0 us
  other arithmetic: 44.3 us -> 0 us
  Pallas kernels: 0 us -> 16.6 us
    slice x60 -> x0, local copies, waits for them, and re-layouts: 113 us -> none  [the longest x59 113 us: shards(): forward = lax.associative_scan(join_pair, (keep, started), axis=1)[1]]
    all_gather x2 -> x0, blocking collectives: 63 us -> none  [carried_in(): gathered = jax.tree.map(lambda a: lax.all_gather(a, axis), part)]
    pad x18 -> x0, local copies, waits for them, and re-layouts: 23.8 us -> none  [shards(): forward = lax.associative_scan(join_pair, (keep, started), axis=1)[1]]
    pallas_call x0 -> x1, Pallas kernels: none -> 16.6 us  [shards(): pl.pallas_call(functools.partial(kernel, n_sp, n_tp, length * n_sp), out_...]
    mul x9 -> x0, other arithmetic: 10.6 us -> none  [the longest x8 10.5 us: join_pair(): return (earlier[0] * later[0], later[0] * earlier[1] + later[1])]
    reduce_sum x2 -> x0, other arithmetic: 10.5 us -> none  [the longest x1 7.26 us: shards(): jnp.sum(gated * gated, axis=-1, keepdims=True)]
    psum x1 -> x0, blocking collectives: 10.1 us -> none  [shards(): lax.psum(jnp.sum(gated * gated, axis=-1, keepdims=True), 'tp')]
    add x19 -> x0, other arithmetic: 8.79 us -> none  [the longest x9 5.34 us: join_pair(): return (earlier[0] * later[0], later[0] * earlier[1] + later[1])]
where the time goes in v1:
time: 19.8 us; the launch traced here: 19.7 us
  Pallas kernels  16.6 us (84%)
  local copies, waits for them, and re-layouts  3.05 us (15%)
    pallas_call x1, Pallas kernels, shards(): pl.pallas_call(functools.partial(kernel, n_sp, n_tp, length * n_sp), out_...  16.6 us
    unnamed x1, local copies, waits for them, and re-layouts  3.05 us

profile of v1, /device:TPU:0, one launch (start us, length us, event | category | flops | bytes accessed | tf_op | source)
XLA Modules:
  0.0 19.7 jit_solution(12444578911232102746)
XLA Ops:
  0.0 16.6 %shard_map.46 = bf16[4,1024,256]{2,1,0:T(8,128)(2,1)} custom-call(f32[4,1024,256]{2,1,0:T(8,128)} %decay_hbm.1, bf16[4,1024,256]{2,1,0:T(8,128)(2,1)} %drive_hbm.1, bf16[4,1024,256]{2,1,0:T(8,128)(2,1)} %gate_hbm.1, f32[1,256]{1,0:T(1,128)} %bitcast.1), custom_call_target="tpu_custom_call" | custom-call | tf_op jit(solution)/shard_map/pallas_call | solution.py:188
  16.6 3.0 %copy.6 = bf16[4,1024,256]{2,1,0:T(8,128)(2,1)} copy(bf16[4,1024,256]{2,1,0:T(8,128)(2,1)} %shard_map.46) | data formatting | bytes 4194304

commit v2 on v1

--- a/solution.py
+++ b/solution.py
@@ -18,10 +18,10 @@
 
 
 def kernel(
-    n_sp, n_tp, total_length, decay_hbm, drive_hbm, gate_hbm, gain_ref, out_hbm,
-    decay, drive, gate, sums, out, chunk_keep, chunk_state,
+    n_sp, n_tp, total_length, decay_hbm, drive_hbm, gate_hbm, gain_hbm, out,
+    decay, drive, gate, gain_ref, sums, chunk_keep, chunk_state,
     mine, gathered, my_power, powers,
-    in_sem, out_sem, sp_send, sp_recv, tp_send, tp_recv,
+    in_sem, gain_sem, sp_send, sp_recv, tp_send, tp_recv,
 ):
     batch, length, channels = decay.shape
     chunks = length // CHUNK
@@ -30,9 +30,6 @@
     def load(b, which):
         src, dst = ((decay_hbm, decay), (drive_hbm, drive), (gate_hbm, gate))[which]
         return pltpu.make_async_copy(src.at[b], dst.at[b], in_sem.at[which, b])
-
-    def store(b):
-        return pltpu.make_async_copy(out.at[b], out_hbm.at[b], out_sem.at[b])
 
     def to_later(j, b):
         return pltpu.make_async_remote_copy(
@@ -60,6 +57,8 @@
         load(b, 1).start()
     for b in range(batch):
         load(b, 2).start()
+    gain_load = pltpu.make_async_copy(gain_hbm, gain_ref, gain_sem)
+    gain_load.start()
 
     barrier = pltpu.get_barrier_semaphore()
 
@@ -147,6 +146,7 @@
 
     lax.fori_loop(0, batch, join_batch, 0)
 
+    gain_load.wait()
     gain = gain_ref[...]
 
     def norm_batch(b, _):
@@ -161,14 +161,11 @@
         for k in range(chunks):
             at = pl.ds(k * CHUNK, CHUNK)
             out[b, at] = (sums[b, at] * scale[:, k : k + 1] * gain).astype(jnp.bfloat16)
-        store(b).start()
         return 0
 
     lax.fori_loop(0, batch, norm_batch, 0)
 
     for b in range(batch):
-        store(b).wait()
-
         def sent(i, _):
             to_later(n_sp - 1 - i, b).wait_send()
             return 0
@@ -176,6 +173,16 @@
         lax.fori_loop(0, n_sp - 1 - sp, sent, 0)
         for i in range(1, n_tp):
             to_peer(i, b).wait_send()
+
+
+def put_kernel(held, out_hbm, sem):
+    copies = [
+        pltpu.make_async_copy(held.at[b], out_hbm.at[b], sem.at[b]) for b in range(held.shape[0])
+    ]
+    for copy in copies:
+        copy.start()
+    for copy in copies:
+        copy.wait()
 
 
 def solution(mesh):
@@ -185,18 +192,17 @@
         batch, length, channels = decay_rate.shape
         chunks = length // CHUNK
         f32 = jnp.float32
-        return pl.pallas_call(
+        held = pl.pallas_call(
             functools.partial(kernel, n_sp, n_tp, length * n_sp),
-            out_shape=jax.ShapeDtypeStruct((batch, length, channels), jnp.bfloat16),
-            in_specs=[pl.BlockSpec(memory_space=pl.ANY)] * 3
-            + [pl.BlockSpec(memory_space=pltpu.VMEM)],
-            out_specs=pl.BlockSpec(memory_space=pl.ANY),
+            out_shape=pltpu.VMEM((batch, length, channels), jnp.bfloat16),
+            in_specs=[pl.BlockSpec(memory_space=pltpu.HBM)] * 4,
+            out_specs=pl.BlockSpec(memory_space=pltpu.VMEM),
             scratch_shapes=[
                 pltpu.VMEM((batch, length, channels), f32),
                 pltpu.VMEM((batch, length, channels), jnp.bfloat16),
                 pltpu.VMEM((batch, length, channels), jnp.bfloat16),
+                pltpu.VMEM((1, channels), f32),
                 pltpu.VMEM((batch, length, channels), f32),
-                pltpu.VMEM((batch, length, channels), jnp.bfloat16),
                 pltpu.VMEM((batch, chunks, channels), f32),
                 pltpu.VMEM((batch, chunks, channels), f32),
                 pltpu.VMEM((batch, 2, channels), f32),
@@ -204,7 +210,7 @@
                 pltpu.VMEM((batch, chunks, CHUNK), f32),
                 pltpu.VMEM((n_tp - 1, batch, chunks, CHUNK), f32),
                 pltpu.SemaphoreType.DMA((3, batch)),
-                pltpu.SemaphoreType.DMA((batch,)),
+                pltpu.SemaphoreType.DMA,
                 pltpu.SemaphoreType.DMA((n_sp, batch)),
                 pltpu.SemaphoreType.DMA((n_sp, batch)),
                 pltpu.SemaphoreType.DMA((n_tp - 1, batch)),
@@ -212,6 +218,14 @@
             ],
             compiler_params=pltpu.CompilerParams(collective_id=0, has_side_effects=True),
         )(decay_rate, drive_in, gate_in, norm_gain.reshape(1, channels))
+        return pl.pallas_call(
+            put_kernel,
+            out_shape=jax.ShapeDtypeStruct(held.shape, held.dtype),
+            in_specs=[pl.BlockSpec(memory_space=pl.ANY)],
+            out_specs=pl.BlockSpec(memory_space=pltpu.HBM),
+            scratch_shapes=[pltpu.SemaphoreType.DMA((batch,))],
+            compiler_params=pltpu.CompilerParams(vmem_limit_bytes=4 * 2**20),
+        )(held)
 
     placed = (P(None, "sp", "tp"), P(None, "sp", "tp"), P(None, "sp", "tp"), P("tp"))
     return jax.shard_map(

time: 19.8 us -> 17 us (0.86)
  local copies, waits for them, and re-layouts: 3.05 us -> 0 us
  Pallas kernels: 16.6 us -> 16.8 us
    unnamed x1 -> x0, local copies, waits for them, and re-layouts: 3.05 us -> none
    pallas_call x0 -> x1, Pallas kernels: none -> 1.35 us  [shards(): pl.pallas_call(put_kernel, out_shape=jax.ShapeDtypeStruct(held.shape, hel...]
    pallas_call x1, Pallas kernels: 16.6 us -> 15.5 us  [shards(): pl.pallas_call(functools.partial(kernel, n_sp, n_tp, length * n_sp), out_...]
where the time goes in v2:
time: 17 us; the launch traced here: 16.8 us
  Pallas kernels  16.8 us (99%)
    pallas_call x1, Pallas kernels, shards(): pl.pallas_call(functools.partial(kernel, n_sp, n_tp, length * n_sp), out_...  15.5 us
    pallas_call x1, Pallas kernels, shards(): pl.pallas_call(put_kernel, out_shape=jax.ShapeDtypeStruct(held.shape, hel...  1.35 us

profile of v2, /device:TPU:0, one launch (start us, length us, event | category | flops | bytes accessed | tf_op | source)
XLA Modules:
  0.0 16.8 jit_solution(603229495518057155)
XLA Ops:
  0.0 15.5 %shard_map.46.held = bf16[4,1024,256]{2,1,0:T(8,128)(2,1)S(1)} custom-call(f32[4,1024,256]{2,1,0:T(8,128)} %decay_hbm.1, bf16[4,1024,256]{2,1,0:T(8,128)(2,1)} %drive_hbm.1, bf16[4,1024,256]{2,1,0:T(8,128)(2,1)} %gate_hbm.1, f32[1,256]{1,0:T(1,128)} %bitcast.1), custom_call_target="tpu_custom_call" | custom-call | tf_op jit(solution)/shard_map/pallas_call | solution.py:195
  15.5 1.3 %shard_map.47 = bf16[4,1024,256]{2,1,0:T(8,128)(2,1)} custom-call(bf16[4,1024,256]{2,1,0:T(8,128)(2,1)S(1)} %shard_map.46.held), custom_call_target="tpu_custom_call" | custom-call | tf_op jit(solution)/shard_map/pallas_call | solution.py:221

commit v3 on v2

--- a/solution.py
+++ b/solution.py
@@ -88,14 +88,14 @@
         for k in range(chunks):
             at = pl.ds(k * CHUNK, CHUNK)
             passed = running(decay[b, at]) * (1.0 / total_length)
-            summed = running(jnp.exp(passed) * drive[b, at].astype(jnp.float32))
+            pushed = jnp.exp(passed) * drive[b, at].astype(jnp.float32)
             fall = jnp.exp(-passed)
             decay[b, at] = fall
-            sums[b, at] = summed
+            sums[b, at] = pushed
             chunk_keep[b, pl.ds(k, 1)] = keep
             chunk_state[b, pl.ds(k, 1)] = state
             last = fall[CHUNK - 1 :]
-            state = last * (state + summed[CHUNK - 1 :])
+            state = last * (state + jnp.sum(pushed, axis=0, keepdims=True))
             keep = last * keep
         mine[b, pl.ds(0, 1)] = keep
         mine[b, pl.ds(1, 1)] = state
@@ -119,7 +119,7 @@
             at = pl.ds(k * CHUNK, CHUNK)
             opened = decay[b, at] * (1.0 + jnp.tanh(0.5 * gate[b, at].astype(jnp.float32)))
             decay[b, at] = opened
-            sums[b, at] = opened * sums[b, at]
+            sums[b, at] = opened * running(sums[b, at])
         return 0
 
     lax.fori_loop(0, batch, gate_batch, 0)

time: 17 us -> 16.9 us (level)
  no operation moved by 1% of the time
where the time goes in v3:
time: 16.9 us; the launch traced here: 16.8 us
  Pallas kernels  16.8 us (99%)
    pallas_call x1, Pallas kernels, shards(): pl.pallas_call(functools.partial(kernel, n_sp, n_tp, length * n_sp), out_...  15.4 us
    pallas_call x1, Pallas kernels, shards(): pl.pallas_call(put_kernel, out_shape=jax.ShapeDtypeStruct(held.shape, hel...  1.35 us

profile of v3, /device:TPU:0, one launch (start us, length us, event | category | flops | bytes accessed | tf_op | source)
XLA Modules:
  0.0 16.8 jit_solution(1812367816568547901)
XLA Ops:
  0.0 15.4 %shard_map.46.held = bf16[4,1024,256]{2,1,0:T(8,128)(2,1)S(1)} custom-call(f32[4,1024,256]{2,1,0:T(8,128)} %decay_hbm.1, bf16[4,1024,256]{2,1,0:T(8,128)(2,1)} %drive_hbm.1, bf16[4,1024,256]{2,1,0:T(8,128)(2,1)} %gate_hbm.1, f32[1,256]{1,0:T(1,128)} %bitcast.1), custom_call_target="tpu_custom_call" | custom-call | tf_op jit(solution)/shard_map/pallas_call | solution.py:195
  15.4 1.3 %shard_map.47 = bf16[4,1024,256]{2,1,0:T(8,128)(2,1)} custom-call(bf16[4,1024,256]{2,1,0:T(8,128)(2,1)S(1)} %shard_map.46.held), custom_call_target="tpu_custom_call" | custom-call | tf_op jit(solution)/shard_map/pallas_call | solution.py:221
